TPU v7x, 256 devices: a 8x8x2 block of a 8x8x16 slice. The times are simulated.
256 devices in a mesh: grp: 2 (over z), kvp: 16 (over x, core), tp: 8 (over y).
Axes of the slice: x: 8, y: 8, z: 2, core: 2. Of those that a mesh axis runs over, the one named last changes fastest.
The devices are a block of a 8x8x16 slice.
Arguments:
- hidden_in: bfloat16 [16, 7168], P('grp'), parts along dimension 0, may hold values from -3 to 3
- queries_nope: bfloat16 [16, 128, 128], P('grp', ('kvp', 'tp')), parts along dimension 0, may hold values from -6 to 6
- queries_rope: bfloat16 [16, 128, 64], P('grp', ('kvp', 'tp')), parts along dimension 0, may hold values from -26 to 26
- cache: bfloat16 [16, 6144, 576], P('grp', 'kvp'), parts along dimension 0, may hold values from -20 to 20
- lengths: int32 [16], P('grp'), parts along dimension 0, may hold values from 128 to 6144, as said below
- w_uk: bfloat16 [128, 128, 512], P(('kvp', 'tp')), may hold values from -0.5 to 0.5
- w_uv: bfloat16 [128, 512, 128], P(('kvp', 'tp')), may hold values from -0.25 to 0.25
- w_out: bfloat16 [16384, 7168], P(('kvp', 'tp')), may hold values from -0.1875 to 0.1875
- norm_gain: float32 [7168], replicated, may hold values from 0.25 to 1.75
- w_gate: bfloat16 [7168, 18432], P(None, ('kvp', 'tp')), may hold values from -0.0625 to 0.0625
- w_up: bfloat16 [7168, 18432], P(None, ('kvp', 'tp')), may hold values from -0.0625 to 0.0625
- w_down: bfloat16 [18432, 7168], P(('kvp', 'tp')), may hold values from -0.15625 to 0.15625
Outputs:
- layer_out: bfloat16 [16, 7168], P('grp', ('kvp', 'tp')), parts along dimension 0
There are 2 independent parts, one for each index of `grp`. A program takes and returns all parts, laid end to end along the dimension named above; an argument that names none is the same for every part. Nothing has to cross between parts.
Inputs may be any that keep to these rules, and one draw needn't show every extreme that they name: `lengths`: every length is a multiple of 128; in every draw some request has the full 6144.
All inputs are finite; a program needn't handle non-finite values.
Results may differ from a plain program's by a relative error of at most 0.04.
Values may be sent and summed in bfloat16 or wider, within the bound.
A program may use at most 64 MiB of HBM per device.

v0:
```python
import jax
import jax.numpy as jnp
from jax import lax
from jax.sharding import Mesh
from jax.sharding import PartitionSpec as P

KVP = ("kvp_0", "kvp_1")
KVP_TP = ("kvp_0", "kvp_1", "tp")


def in_one_piece(arrays, axis, dim, along):
    both = jnp.concatenate(arrays, axis=along)
    whole, at, gathered = (lax.all_gather(both, axis, axis=dim, tiled=True), 0, [])
    for a in arrays:
        gathered.append(lax.slice_in_dim(whole, at, at + a.shape[along], axis=along))
        at += a.shape[along]
    return tuple(gathered)


def sum_in_order(blocks, axes, sequence):
    inside = blocks.shape[1:]
    blocks = blocks.reshape(*(lax.axis_size(a) for a in axes), *inside)
    blocks = jnp.moveaxis(blocks, sequence, range(len(axes))).reshape(-1, *inside)
    for k in sequence:
        blocks = lax.psum_scatter(blocks, axes[k], scatter_dimension=0, tiled=True)
    return blocks[0]


def in_blocks(value, dim, size):
    dims = value.shape
    blocks = value.reshape(*dims[:dim], size, dims[dim] // size, *dims[dim + 1 :])
    return jnp.moveaxis(blocks, dim, 0)


def sum_by_axis(value, axes, sequence, dim):
    size = lax.axis_size(axes)
    return sum_in_order(in_blocks(value, dim, size), axes, sequence)


def project(o_lat, w_uv, w_out):
    head_out = jnp.einsum("bhl,hle->bhe", o_lat, w_uv, preferred_element_type=jnp.float32).astype(
        jnp.bfloat16
    )
    return jnp.dot(
        head_out.reshape(head_out.shape[0], -1), w_out, preferred_element_type=jnp.float32
    )


def per_device(
    hidden_in,
    queries_nope,
    queries_rope,
    cache,
    lengths,
    w_uk,
    w_uv,
    w_out,
    norm_gain,
    w_gate,
    w_up,
    w_down,
):
    batch, heads_dev, head_dim = queries_nope.shape
    latent = w_uk.shape[2]
    ctx_dev = cache.shape[1]
    groups = lax.axis_size(KVP)
    score_scale = float(head_dim + queries_rope.shape[2]) ** (-0.5)
    q_lat = jnp.einsum(
        "bhd,hdl->bhl", queries_nope, w_uk, preferred_element_type=jnp.float32
    ).astype(jnp.bfloat16)
    q_lat_all, rope_all = in_one_piece((q_lat, queries_rope), KVP, 1, 2)
    q_full = jnp.concatenate([q_lat_all, rope_all], axis=2)
    scores = (
        jnp.einsum("bhc,btc->bht", q_full, cache, preferred_element_type=jnp.float32) * score_scale
    )
    offset = lax.axis_index(KVP) * ctx_dev
    visible = ((offset + jnp.arange(ctx_dev, dtype=jnp.int32))[None, :] < lengths[:, None])[
        :, None, :
    ]
    masked = jnp.where(visible, scores, jnp.float32(-1e30))
    block_max = jnp.max(masked, axis=2)
    exponent = jnp.where(visible, jnp.exp(masked - block_max[..., None]), jnp.float32(0.0))
    guarded = jnp.maximum(jnp.sum(exponent, axis=2), 1.0)
    log_total = block_max + jnp.log(guarded)
    weights = (exponent / guarded[..., None]).astype(jnp.bfloat16)
    partial_value = jnp.einsum("bht,btc->bhc", weights, cache, preferred_element_type=jnp.float32)[
        ..., :latent
    ]
    blocks = partial_value.reshape(batch, groups, heads_dev, latent)
    block_logs = log_total.reshape(batch, groups, heads_dev)
    part_blocks = lax.all_to_all(
        blocks.astype(jnp.bfloat16), KVP, split_axis=1, concat_axis=1, tiled=True
    ).astype(blocks.dtype)
    part_logs = lax.all_to_all(
        block_logs.astype(jnp.bfloat16), KVP, split_axis=1, concat_axis=1, tiled=True
    ).astype(block_logs.dtype)
    highest = jnp.max(part_logs, axis=1)
    overall = highest + jnp.log(jnp.sum(jnp.exp(part_logs - highest[:, None, :]), axis=1))
    scaled = jnp.exp(part_logs - overall[:, None, :])[..., None] * part_blocks
    o_lat = jnp.sum(scaled, axis=1).astype(jnp.bfloat16)
    attention = project(o_lat, w_uv, w_out)
    model_width = norm_gain.shape[0]
    share_width = model_width // lax.axis_size(KVP_TP)
    share_start = lax.axis_index(KVP_TP) * share_width
    attn_whole = lax.psum(attention, KVP_TP)
    residual = hidden_in.astype(jnp.float32) + attn_whole
    mean_square = jnp.mean(residual * residual, axis=1)
    normed = (residual * lax.rsqrt(mean_square + 1e-06)[:, None] * norm_gain[None, :]).astype(
        jnp.bfloat16
    )
    residual_share = lax.dynamic_slice_in_dim(residual, share_start, share_width, 1)
    gate_proj = jnp.dot(normed, w_gate, preferred_element_type=jnp.float32)
    up_proj = jnp.dot(normed, w_up, preferred_element_type=jnp.float32)
    act = (jax.nn.silu(gate_proj) * up_proj).astype(jnp.bfloat16)
    ffn_terms = jnp.dot(act, w_down, preferred_element_type=jnp.float32)
    ffn_share = sum_by_axis(ffn_terms, KVP_TP, (1, 0, 2), 1)
    return (residual_share + ffn_share).astype(jnp.bfloat16)


def solution(mesh):
    torus = Mesh(
        mesh.devices.reshape(mesh.shape["grp"], 8, 2, mesh.shape["tp"]),
        ("grp", "kvp_0", "kvp_1", "tp"),
    )
    return jax.shard_map(
        per_device,
        mesh=torus,
        in_specs=(
            P("grp", None),
            P("grp", KVP_TP, None),
            P("grp", KVP_TP, None),
            P("grp", KVP, None),
            P("grp"),
            P(KVP_TP, None, None),
            P(KVP_TP, None, None),
            P(KVP_TP, None),
            P(),
            P(None, KVP_TP),
            P(None, KVP_TP),
            P(KVP_TP, None),
        ),
        out_specs=P("grp", KVP_TP),
        check_vma=False,
    )
```

profile of v0, /device:TPU:514, one launch (start us, length us, event | category | flops | bytes accessed | tf_op | source)
XLA Modules:
  0.0 365.7 jit_solution(1368219524394948218)
XLA Ops:
  6.5 0.0 copy-start
  6.6 1.2 fusion.1
  7.7 0.7 pad_maximum_fusion
  8.4 34.0 %all_gather.3 = bf16[8,16,576]{2,0,1:T(8,128)(2,1)S(1)} all-gather(bf16[8,1,576]{2,0,1:T(8,128)(2,1)S(1)} %pad_maximum_fusion), channel_id=1, replica_groups=mesh['grp'=2,'kvp_0'=8,'kvp_1'=2,'tp'=8] {'kvp_0','kvp_1'}, dimensions={1}, use_global_device_ids=true | all-gather | bytes 156672 | tf_op jit(solution)/shard_map/all_gather | solution.py:13
  42.4 0.7 broadcast_compare_fusion
  43.1 0.0 copy-done
  43.1 0.7 fusion.35
  43.8 0.0 copy-start.2
  43.8 0.7 copy-done.2
  44.5 0.2 fusion.6
  44.7 0.6 fusion.30
  45.3 0.7 copy.24
  45.9 3.6 all-to-all-start
  49.5 2.0 fusion.11
  51.6 0.7 copy.27
  52.3 3.4 all-to-all-done
  55.7 5.4 %all-to-all-start.1 = ((bf16[8,16,1,512]{3,0,2,1:T(8,128)(2,1)}), bf16[8,16,1,512]{3,0,2,1:T(8,128)(2,1)}, u32[]{:S(2)}, u32[]{:S(2)}) async-start(bf16[8,16,1,512]{3,0,2,1:T(8,128)(2,1)} %copy.27), calls=%async_computation.1 | async-start | bytes 262144 | tf_op jit(solution)/shard_map/all_to_all | solution.py:91
  61.1 0.1 all-reduce.3.cloned.1.call-start
  61.2 0.5 reduce_max.25
  61.7 0.1 copy.25
  61.8 0.8 fusion.24
  62.6 0.1 fusion.26
  62.7 0.1 copy.26
  62.8 5.9 %all-to-all-done.1 = bf16[8,16,1,512]{3,0,2,1:T(8,128)(2,1)} async-done(((bf16[8,16,1,512]{3,0,2,1:T(8,128)(2,1)}), bf16[8,16,1,512]{3,0,2,1:T(8,128)(2,1)}, u32[]{:S(2)}, u32[]{:S(2)}) %all-to-all-start.1) | async-done | bytes 131104 | tf_op jit(solution)/shard_map/all_to_all | solution.py:91
  68.7 1.0 multiply_reduce_fusion
  69.7 2.7 fusion.4
  72.4 0.1 all-reduce.3.cloned.1.call-update
  72.5 0.1 reduce-scatter.3.cloned.1.call-start
  72.5 185.7 %all-reduce.3.cloned.1.call-done = f32[8,7168]{1,0:T(8,128)} async-done(((f32[8,7168]{1,0:T(8,128)}), f32[8,7168]{1,0:T(8,128)}) %all-reduce.3.cloned.1.call-update) | async-done | bytes 229392 | tf_op jit(solution)/shard_map/psum | solution.py:105
  258.3 1.2 multiply_reduce_fusion.1
  259.5 0.0 copy-start.1
  259.5 0.7 copy-done.1
  260.2 2.3 fusion.34
  262.4 4.6 %fusion.3 = f32[8,7168]{1,0:T(8,128)} fusion(bf16[144,7168]{1,0:T(8,128)(2,1)} %param.23, bf16[7168,144]{0,1:T(8,128)(2,1)} %param.22, f32[8,144]{1,0:T(8,128)S(1)} %fusion.34, f32[8,7168]{1,0:T(8,128)} %copy-done.1, f32[7168]{0:T(1024)} %param.20, f32[8]{0:T(128)S(1)} %add_rsqrt_fusion), kind=kOutput, calls=%fused_computation.6 | convolution fusion | flops 33209088 | bytes 4620832 | tf_op jit(solution)/shard_map/dot_general | solution.py:115
  267.1 0.0 copy-start.3
  267.1 2.2 reshape.125
  269.3 2.2 copy.29
  271.4 0.1 reduce-scatter.3.cloned.1.call-update
  271.5 0.1 reduce-scatter.5.cloned.1.call-start
  271.5 12.6 %reduce-scatter.3.cloned.1.call-done = f32[64,8,56]{2,1,0:T(8,128)} async-done(((f32[128,8,56]{2,1,0:T(8,128)}), f32[64,8,56]{2,1,0:T(8,128)}) %reduce-scatter.3.cloned.1.call-update) | async-done | bytes 114704 | tf_op jit(solution)/shard_map/reduce_scatter | solution.py:25
  284.2 0.1 reduce-scatter.5.cloned.1.call-update
  284.3 0.0 copy-done.3
  284.3 0.6 dynamic-slice
  284.8 41.0 %reduce-scatter.5.cloned.1.call-done = f32[8,8,56]{2,1,0:T(8,128)} async-done(((f32[64,8,56]{2,1,0:T(8,128)}), f32[8,8,56]{2,1,0:T(8,128)}) %reduce-scatter.5.cloned.1.call-update) | async-done | bytes 14352 | tf_op jit(solution)/shard_map/reduce_scatter | solution.py:25
  325.8 31.4 %all-reduce = f32[8,8,56]{2,1,0:T(8,128)} all-reduce(f32[8,8,56]{2,1,0:T(8,128)} %reduce-scatter.5.cloned.1.call-done), channel_id=4, replica_groups=mesh['grp'=2,'kvp_0'=8,'kvp_1'=2,'tp'=8] {'tp'}, use_global_device_ids=true, to_apply=%region_9.10.clone | all-reduce | flops 3584 | bytes 28672
  357.3 1.9 fusion.28
  (5 shorter events, 0.1 us)
Async XLA Ops:
  6.5 36.6 %copy-start = (bf16[8,384,576]{1,2,0:T(8,128)(2,1)S(1)}, bf16[8,384,576]{1,2,0:T(8,128)(2,1)}, u32[]{:S(2)}) copy-start(bf16[8,384,576]{1,2,0:T(8,128)(2,1)} %param.15) | copy-start | bytes 10616836
  43.8 0.7 copy-start.2
  45.9 9.8 %all-to-all-start = ((bf16[8,16,1]{0,2,1:T(2,128)(2,1)}), bf16[8,16,1]{0,2,1:T(2,128)(2,1)S(1)}, u32[]{:S(2)}, u32[]{:S(2)}) async-start(bf16[8,16,1]{0,2,1:T(2,128)(2,1)} %copy.24), calls=%async_computation | async-start | bytes 16384 | tf_op jit(solution)/shard_map/all_to_all | solution.py:94
  55.7 12.9 %all-to-all-start.1 = ((bf16[8,16,1,512]{3,0,2,1:T(8,128)(2,1)}), bf16[8,16,1,512]{3,0,2,1:T(8,128)(2,1)}, u32[]{:S(2)}, u32[]{:S(2)}) async-start(bf16[8,16,1,512]{3,0,2,1:T(8,128)(2,1)} %copy.27), calls=%async_computation.1 | async-start | bytes 262144 | tf_op jit(solution)/shard_map/all_to_all | solution.py:91
  61.1 197.2 %all-reduce.3.cloned.1.call-start = ((), (), s32[]{:S(2)}) async-start(), calls=%async_computation.4 | async-start | bytes 458752 | tf_op jit(solution)/shard_map/psum | solution.py:105
  72.5 211.7 %reduce-scatter.3.cloned.1.call-start = ((), (), s32[]{:S(2)}) async-start(), calls=%async_computation.5 | async-start | bytes 786432 | tf_op jit(solution)/shard_map/reduce_scatter | solution.py:25
  259.5 0.7 copy-start.1
  267.1 17.2 %copy-start.3 = (u32[256]{0:T(256)S(1)}, u32[256]{0:T(256)}, u32[]{:S(2)}) copy-start(u32[256]{0:T(256)} %constant.55) | copy-start | bytes 3076
  271.5 54.4 %reduce-scatter.5.cloned.1.call-start = ((), (), s32[]{:S(2)}) async-start(), calls=%async_computation.6 | async-start | bytes 294912 | tf_op jit(solution)/shard_map/reduce_scatter | solution.py:25
Sparse Core Ops, SparseCore 0:
  72.6 185.6 all-reduce.2
  271.6 12.5 reduce-scatter.2
  286.7 39.0 reduce-scatter.4
where the time goes:
time: 366 us
  waiting for transfers between devices  249 us (68%)
  blocking collectives  65.4 us (18%)
  matrix products  13.5 us (4%)
  between operations  13.2 us (4%)
  starting transfers between devices  9.14 us (2%)
  local copies, waits for them, and re-layouts  7.86 us (2%)
  other arithmetic  7.76 us (2%)
    psum x1, waiting for transfers between devices, per_device(): attn_whole = lax.psum(attention, KVP_TP)  186 us
    reduce_scatter x2, waiting for transfers between devices, sum_in_order(): blocks = lax.psum_scatter(blocks, axes[k], scatter_dimension=0, tiled=True)  53.6 us
    all_gather x1, blocking collectives, in_one_piece(): lax.all_gather(both, axis, axis=dim, tiled=True)  34 us
    unnamed x1, blocking collectives  31.4 us
  transfers between devices with their start and end apart: 5, of which 5 were waited for; matrix products, arithmetic and copies ran while one was open for 1% of the time, Pallas kernels for 0%

commit v1 on v0

v1 whole, which is shorter than its diff:
```python
import functools

import jax
import jax.numpy as jnp
from jax import lax
from jax.experimental import pallas as pl
from jax.experimental.pallas import tpu as pltpu
from jax.sharding import PartitionSpec as P

MESH = pl.DeviceIdType.MESH
BF16 = jnp.bfloat16
F32 = jnp.float32
LANES = 128
CORES = 2


def rows_of(core, first, second):
    return jnp.where(core == 0, first, second)


def kernel(
    n_kvp,
    n_tp,
    hidden_hbm,
    qn_hbm,
    qr_hbm,
    cache_hbm,
    lengths_hbm,
    wuk_hbm,
    wuv_hbm,
    wout_hbm,
    gain_hbm,
    wg_hbm,
    wu_hbm,
    wd_hbm,
    out_ref,
    hidden,
    qn,
    qr,
    cache,
    lengths,
    wuk,
    wuv,
    wout,
    gain,
    wg,
    wu,
    wd,
    qbuf,
    psend,
    pbuf,
    d1_mine,
    d1_send,
    d1_recv,
    rs1_send,
    rs1_recv,
    ag_own,
    ag_other,
    res,
    d2_mine,
    d2_send,
    d2_recv,
    rs2_send,
    rs2_recv,
    sw_send,
    sw_recv,
    load_sem,
    send_sem,
    recv_sem,
    sync_sem,
):
    k = lax.axis_index("kvp")
    t = lax.axis_index("tp")
    x, c = k // CORES, k % CORES
    n_x = n_kvp // CORES
    n_chips = n_x * n_tp
    batch, width = hidden.shape
    half = batch // 2
    latent = wuk.shape[1]
    rope = qr.shape[1]
    ctx_dev = cache.shape[2]
    n_tiles = width // LANES
    share = width // (n_kvp * n_tp)
    chip = x * n_tp + t
    per_row = n_tiles // n_x

    def device(px, pc, py):
        return {"kvp": px * CORES + pc, "tp": py}

    def load(i, src, dst):
        copy = pltpu.make_async_copy(src, dst, load_sem.at[i])
        copy.start()
        return copy

    l_qn = load(0, qn_hbm, qn)
    l_wuk = load(1, wuk_hbm, wuk)
    l_qr = load(2, qr_hbm, qr)
    l_len = load(3, lengths_hbm, lengths)
    l_cache = load(4, cache_hbm, cache)
    l_wuv = load(5, wuv_hbm, wuv)
    l_wout = load(6, wout_hbm, wout)
    l_hidden = load(7, hidden_hbm, hidden)
    l_gain = load(8, gain_hbm, gain)
    l_wg = load(9, wg_hbm, wg)
    l_wu = load(10, wu_hbm, wu)
    l_wd = load(11, wd_hbm, wd)

    barrier = pltpu.get_barrier_semaphore()
    for i in range(1, n_kvp):
        pl.semaphore_signal(
            barrier, inc=1, device_id={"kvp": (k + i) % n_kvp, "tp": t}, device_id_type=MESH
        )
    for i in range(1, n_tp):
        pl.semaphore_signal(
            barrier, inc=1, device_id={"kvp": k, "tp": (t + i) % n_tp}, device_id_type=MESH
        )

    l_qn.wait()
    l_wuk.wait()
    l_qr.wait()
    q_lat = jnp.dot(qn[...], wuk[...], preferred_element_type=F32).astype(BF16)
    qbuf[k, :, :latent] = q_lat
    qbuf[k, :, latent:] = jnp.concatenate(
        [qr[...], jnp.zeros((batch, qbuf.shape[2] - latent - rope), BF16)], axis=1
    )
    pl.semaphore_wait(barrier, n_kvp - 1 + n_tp - 1)

    order = sorted(range(1, n_kvp), key=lambda i: abs(i - n_kvp // 2))

    def to_kvp(src, dst, phase):
        for i in order:
            peer = (k + i) % n_kvp
            pltpu.make_async_remote_copy(
                src(peer),
                dst,
                send_sem.at[phase],
                recv_sem.at[phase],
                device_id={"kvp": peer, "tp": t},
                device_id_type=MESH,
            ).start()

    def bulk(ref, phase):
        return pltpu.make_async_remote_copy(
            ref,
            ref,
            send_sem.at[phase],
            recv_sem.at[phase],
            device_id=device(x, 1 - c, t),
            device_id_type=MESH,
        )

    to_kvp(lambda peer: qbuf.at[k], qbuf.at[k], 0)
    for i in range(1, n_tp):
        pl.semaphore_signal(
            sync_sem, inc=1, device_id={"kvp": k, "tp": (t + i) % n_tp}, device_id_type=MESH
        )

    l_len.wait()
    row = lax.broadcasted_iota(jnp.int32, (batch, ctx_dev), 0)
    position = lax.broadcasted_iota(jnp.int32, (batch, ctx_dev), 1) + k * ctx_dev
    length = jnp.zeros((batch, ctx_dev), jnp.int32)
    for b in range(batch):
        length = jnp.where(row == b, lengths[b], length)
    visible = (position < length)[None]
    row = row[None]
    l_cache.wait()
    bulk(qbuf.at[pl.ds(0, n_kvp - 1)], 0).wait_recv()

    rows = n_kvp * batch
    queries = qbuf[...].astype(F32).reshape(rows, qbuf.shape[2]).astype(BF16)
    queries = queries[:, : latent + rope]
    scale = float(qn.shape[1] + rope) ** (-0.5)
    scores = jnp.zeros((n_kvp, batch, ctx_dev), F32)
    for b in range(batch):
        s_b = jnp.dot(queries, cache[b], preferred_element_type=F32)
        scores = jnp.where(row == b, s_b.reshape(n_kvp, batch, ctx_dev), scores)
    masked = jnp.where(visible, scores * scale, F32(-1e30))
    block_max = jnp.max(masked, axis=2, keepdims=True)
    exps = jnp.where(visible, jnp.exp(masked - block_max), F32(0.0))
    guarded = jnp.maximum(jnp.sum(exps, axis=2, keepdims=True), 1.0)
    log_total = block_max + jnp.log(guarded)
    weights = exps / guarded
    partial = jnp.zeros((rows, latent), F32)
    for b in range(batch):
        w_b = jnp.where(row == b, weights, F32(0.0)).reshape(rows, ctx_dev).astype(BF16)
        partial += lax.dot_general(
            w_b, cache[b, :latent, :], (((1,), (1,)), ((), ())), preferred_element_type=F32
        )
    log_high = log_total.astype(BF16).astype(F32)
    log_low = log_total - log_high
    lane = lax.broadcasted_iota(jnp.int32, (n_kvp, batch, LANES), 2)
    logs = jnp.where(lane == 0, log_high, jnp.where(lane == 1, log_low, F32(0.0)))
    psend[:, :, :latent] = partial.reshape(n_kvp, batch, latent).astype(BF16)
    psend[:, :, latent:] = logs.astype(BF16)
    pbuf[k] = psend[k]
    to_kvp(lambda peer: psend.at[peer], pbuf.at[k], 1)
    l_wuv.wait()
    l_wout.wait()
    bulk(pbuf.at[pl.ds(0, n_kvp - 1)], 1).wait_recv()

    parts = pbuf[...].astype(F32)
    part_logs = parts[:, :, latent : latent + 1] + parts[:, :, latent + 1 : latent + 2]
    shifted = jnp.exp(part_logs - jnp.max(part_logs, axis=0, keepdims=True))
    coef = shifted / jnp.sum(shifted, axis=0, keepdims=True)
    o_lat = jnp.sum(coef * parts[:, :, :latent], axis=0).astype(BF16)
    head_out = jnp.dot(o_lat, wuv[...], preferred_element_type=F32).astype(BF16)
    attention = jnp.dot(head_out, wout[...], preferred_element_type=F32)

    for j in range(n_tiles):
        tile = attention[:, j * LANES : (j + 1) * LANES]
        d1_mine[j] = rows_of(c, tile[:half], tile[half:])
        d1_send[j] = rows_of(c, tile[half:], tile[:half]).astype(BF16)

    def swap(src, dst, phase):
        copy = pltpu.make_async_remote_copy(
            src,
            dst,
            send_sem.at[phase],
            recv_sem.at[phase],
            device_id=device(x, 1 - c, t),
            device_id_type=MESH,
        )
        copy.start()
        return copy

    s1 = swap(d1_send, d1_recv, 2)
    s1.wait_recv()
    rs1_send[...] = (d1_mine[...] + d1_recv[...].astype(F32)).astype(BF16)
    pl.semaphore_wait(sync_sem, n_tp - 1)

    def to_chips(start_one):
        def step(i, _):
            px = (x + n_x // 2 + i // n_tp) % n_x
            py = (t + n_tp // 2 + i % n_tp) % n_tp
            start_one(px, py)
            return 0

        middle = (n_x // 2) * n_tp + n_tp // 2
        lax.fori_loop(0, middle, step, 0)
        lax.fori_loop(middle + 1, n_chips, step, 0)

    def slot_of(px, py):
        return (px + py) % n_x, px * per_row + (px + py) % n_x

    my_place, my_tile = slot_of(x, t)
    owner = my_place < per_row

    def rs1_one(px, py):
        place, tile = slot_of(px, py)

        @pl.when(place < per_row)
        def _():
            pltpu.make_async_remote_copy(
                rs1_send.at[tile],
                rs1_recv.at[chip],
                send_sem.at[3],
                recv_sem.at[3],
                device_id=device(px, c, py),
                device_id_type=MESH,
            ).start()

    to_chips(rs1_one)
    l_hidden.wait()

    def ag_one(px, py):
        pltpu.make_async_remote_copy(
            ag_own.at[my_tile],
            ag_own.at[my_tile],
            send_sem.at[4],
            recv_sem.at[4],
            device_id=device(px, c, py),
            device_id_type=MESH,
        ).start()

    @pl.when(owner)
    def _():
        rs1_recv[chip] = rs1_send[my_tile]
        mine = hidden[:, pl.ds(pl.multiple_of(my_tile * LANES, LANES), LANES)].astype(F32)
        mine = rows_of(c, mine[:half], mine[half:])
        bulk(rs1_recv.at[pl.ds(0, n_chips - 1)], 3).wait_recv()
        total = mine + jnp.sum(rs1_recv[...].astype(F32), axis=0)
        ag_own[my_tile] = total.astype(BF16)
        to_chips(ag_one)
        bulk(ag_own.at[pl.ds(0, n_tiles - 1)], 4).wait_recv()

    @pl.when(jnp.logical_not(owner))
    def _():
        bulk(ag_own.at[pl.ds(0, n_tiles)], 4).wait_recv()

    s2 = swap(ag_own, ag_other, 5)
    l_gain.wait()
    l_wg.wait()
    l_wu.wait()
    s2.wait_recv()

    own = ag_own[...].astype(F32)
    other = ag_other[...].astype(F32)
    residual = jnp.concatenate([rows_of(c, own, other), rows_of(c, other, own)], axis=1)
    res[:n_tiles] = residual
    res[n_tiles] = jnp.zeros((batch, LANES), F32)
    squares = jnp.sum(jnp.sum(residual * residual, axis=0), axis=1, keepdims=True)
    inverse = lax.rsqrt(squares / width + 1e-6)
    normed = residual * inverse[None] * gain[...][:, None, :]
    normed = jnp.concatenate([normed[j] for j in range(n_tiles)], axis=1).astype(BF16)
    dims = (((1,), (1,)), ((), ()))
    gate_proj = lax.dot_general(wg[...], normed, dims, preferred_element_type=F32)
    up_proj = lax.dot_general(wu[...], normed, dims, preferred_element_type=F32)
    act = gate_proj / (1.0 + jnp.exp(-gate_proj)) * up_proj
    act = act.T.astype(BF16)
    l_wd.wait()
    ffn = jnp.dot(act, wd[...], preferred_element_type=F32)

    pad = jnp.zeros((batch, LANES - CORES * share), F32)
    for px in range(n_x):
        for py in range(n_tp):
            first = share * (CORES * px * n_tp + py)
            second = first + share * n_tp
            tile = jnp.concatenate(
                [ffn[:, first : first + share], ffn[:, second : second + share], pad], axis=1
            )
            slot = px * n_tp + py
            d2_mine[slot] = rows_of(c, tile[:half], tile[half:])
            d2_send[slot] = rows_of(c, tile[half:], tile[:half]).astype(BF16)
    s3 = swap(d2_send, d2_recv, 6)
    s3.wait_recv()
    rs2_send[...] = (d2_mine[...] + d2_recv[...].astype(F32)).astype(BF16)

    def rs2_one(px, py):
        pltpu.make_async_remote_copy(
            rs2_send.at[px * n_tp + py],
            rs2_recv.at[chip],
            send_sem.at[7],
            recv_sem.at[7],
            device_id=device(px, c, py),
            device_id_type=MESH,
        ).start()

    to_chips(rs2_one)
    rs2_recv[chip] = rs2_send[chip]
    start = share * (k * n_tp + t)
    base = start // LANES
    near = jnp.concatenate([res[base], res[base + 1]], axis=1)
    near = pltpu.roll(near, 2 * LANES - start % LANES, 1)[:, :share]
    bulk(rs2_recv.at[pl.ds(0, n_chips - 1)], 7).wait_recv()
    total = jnp.sum(rs2_recv[...].astype(F32), axis=0)
    sw_send[...] = total
    s4 = swap(sw_send, sw_recv, 8)
    s4.wait_recv()
    peer = sw_recv[...]
    whole = jnp.concatenate([rows_of(c, total, peer), rows_of(c, peer, total)], axis=0)
    mine = rows_of(c, whole[:, :share], whole[:, share : 2 * share])
    out_ref[...] = (near + mine).astype(BF16)

    bulk(qbuf.at[pl.ds(0, n_kvp - 1)], 0).wait_send()
    bulk(pbuf.at[pl.ds(0, n_kvp - 1)], 1).wait_send()
    s1.wait_send()

    @pl.when(owner)
    def _():
        bulk(rs1_send.at[pl.ds(0, n_tiles - 1)], 3).wait_send()
        bulk(rs1_recv.at[pl.ds(0, n_chips - 1)], 4).wait_send()

    @pl.when(jnp.logical_not(owner))
    def _():
        bulk(rs1_send, 3).wait_send()

    s2.wait_send()
    s3.wait_send()
    bulk(rs2_send.at[pl.ds(0, n_chips - 1)], 7).wait_send()
    s4.wait_send()


def per_device(n_kvp, n_tp, *args):
    hidden, qn, qr, cache, lengths, wuk, wuv, wout, gain, wg, wu, wd = args
    batch, width = hidden.shape
    half = batch // 2
    n_chips = n_kvp // CORES * n_tp
    n_tiles = width // LANES
    latent = wuk.shape[2]
    lanes = latent + LANES
    operands = (
        hidden,
        qn.reshape(batch, qn.shape[2]),
        qr.reshape(batch, qr.shape[2]),
        cache.transpose(0, 2, 1),
        lengths,
        wuk.reshape(wuk.shape[1:]),
        wuv.reshape(wuv.shape[1:]),
        wout,
        gain.reshape(n_tiles, LANES),
        wg.T,
        wu.T,
        wd,
    )
    spaces = [pltpu.SMEM if a is lengths else pltpu.VMEM for a in operands]
    share = width // (n_kvp * n_tp)
    return pl.pallas_call(
        functools.partial(kernel, n_kvp, n_tp),
        name="layer",
        out_shape=jax.ShapeDtypeStruct((batch, share), BF16),
        in_specs=[pl.BlockSpec(memory_space=pl.ANY)] * len(operands),
        out_specs=pl.BlockSpec(memory_space=pltpu.VMEM),
        scratch_shapes=[
            *(space(a.shape, a.dtype) for space, a in zip(spaces, operands)),
            pltpu.VMEM((n_kvp, batch, lanes), BF16),
            pltpu.VMEM((n_kvp, batch, lanes), BF16),
            pltpu.VMEM((n_kvp, batch, lanes), BF16),
            pltpu.VMEM((n_tiles, half, LANES), F32),
            pltpu.VMEM((n_tiles, half, LANES), BF16),
            pltpu.VMEM((n_tiles, half, LANES), BF16),
            pltpu.VMEM((n_tiles, half, LANES), BF16),
            pltpu.VMEM((n_chips, half, LANES), BF16),
            pltpu.VMEM((n_tiles, half, LANES), BF16),
            pltpu.VMEM((n_tiles, half, LANES), BF16),
            pltpu.VMEM((n_tiles + 1, batch, LANES), F32),
            pltpu.VMEM((n_chips, half, LANES), F32),
            pltpu.VMEM((n_chips, half, LANES), BF16),
            pltpu.VMEM((n_chips, half, LANES), BF16),
            pltpu.VMEM((n_chips, half, LANES), BF16),
            pltpu.VMEM((n_chips, half, LANES), BF16),
            pltpu.VMEM((half, LANES), F32),
            pltpu.VMEM((half, LANES), F32),
            pltpu.SemaphoreType.DMA((len(operands),)),
            pltpu.SemaphoreType.DMA((9,)),
            pltpu.SemaphoreType.DMA((9,)),
            pltpu.SemaphoreType.REGULAR,
        ],
        compiler_params=pltpu.CompilerParams(
            collective_id=0, has_side_effects=True, vmem_limit_bytes=60 * 1024 * 1024
        ),
    )(*operands)


def solution(mesh):
    n_kvp, n_tp = mesh.shape["kvp"], mesh.shape["tp"]
    both = ("kvp", "tp")
    return jax.shard_map(
        functools.partial(per_device, n_kvp, n_tp),
        mesh=mesh,
        in_specs=(
            P("grp", None),
            P("grp", both, None),
            P("grp", both, None),
            P("grp", "kvp", None),
            P("grp"),
            P(both, None, None),
            P(both, None, None),
            P(both, None),
            P(),
            P(None, both),
            P(None, both),
            P(both, None),
        ),
        out_specs=P("grp", both),
        check_vma=False,
    )
```

time: 366 us -> 70.2 us (0.19)
  the two profiles are of different devices: /device:TPU:514 before, /device:TPU:513 now
where the time goes in v1:
time: 70.2 us; the launch traced here: 70 us
  Pallas kernels  68.8 us (98%)
  local copies, waits for them, and re-layouts  1.26 us (2%)
    pallas_call x1, Pallas kernels, per_device(): pl.pallas_call(functools.partial(kernel, n_kvp, n_tp), name='layer', out_...  68.8 us

profile of v1, /device:TPU:513, one launch (start us, length us, event | category | flops | bytes accessed | tf_op | source)
XLA Modules:
  0.0 70.0 jit_solution(16995695707274779963)
XLA Ops:
  0.0 68.8 %layer.1 = bf16[8,56]{1,0:T(8,128)(2,1)} custom-call(bf16[8,7168]{1,0:T(8,128)(2,1)} %hidden_hbm.1, bf16[8,128]{1,0:T(8,128)(2,1)} %bitcast.14, bf16[8,64]{1,0:T(8,128)(2,1)} %bitcast.15, bf16[8,576,384]{2,1,0:T(8,128)(2,1)} %bitcast.8, s32[8]{0:T(128)} %lengths_hbm.1, bf16[128,512]{1,0:T(8,128)(2,1)} %bitcast.11, bf16[512,128]{1,0:T(8,128)(2,1)} %bitcast.12, ...), custom_call_target="tpu_custom_call" | custom-call | tf_op jit(solution)/shard_map/layer/pallas_call | solution.py:397
  68.8 1.3 %copy.14 = bf16[8,56]{1,0:T(8,128)(2,1)} copy(bf16[8,56]{1,0:T(8,128)(2,1)} %layer.1) | data formatting | bytes 1792
